TPU v7x, 32 devices: a whole 2x2x4 slice. The times are simulated.
32 devices in a mesh: seq: 8 (over z, core), head: 4 (over y, x).
Axes of the slice: x: 2, y: 2, z: 4, core: 2. Of those that a mesh axis runs over, the one named last changes fastest.
Arguments:
- queries: bfloat16 [4096, 16, 128], P(('seq', 'head')), may hold values from -6 to 6
- keys: bfloat16 [4096, 16, 128], P(('seq', 'head')), may hold values from -6 to 6
- values: bfloat16 [4096, 16, 128], P(('seq', 'head')), may hold values from -6 to 6
- beta: float32 [4096, 16], P(('seq', 'head')), may hold values from 0 to 1
- log_decay: float32 [4096, 16], P(('seq', 'head')), may hold values from -1 to 0
- out_gate: bfloat16 [4096, 16, 128], P(('seq', 'head')), may hold values from -6 to 6
- norm_gain: float32 [128], replicated, may hold values from 0.1 to 1.9
Outputs:
- gated_out: bfloat16 [4096, 16, 128], P('seq', 'head')
All inputs are finite; a program needn't handle non-finite values.
Results may differ from a plain program's by a relative error of at most 0.001.
Values may be sent and summed in bfloat16 or wider, within the bound.
A program may use at most 64 MiB of HBM per device.

v0:
```python
import jax
import jax.numpy as jnp
from jax import lax
from jax.sharding import PartitionSpec as P

BLOCK = 128


HIGHEST_PREC = lax.Precision.HIGHEST


def entering(part, axis, combine, identity):
    place = lax.axis_index(axis)
    gathered = jax.tree.map(lambda a: lax.all_gather(a, axis), part)
    state = jax.tree.map(lambda a, e: jnp.zeros_like(a) + jnp.asarray(e, a.dtype), part, identity)

    def one(lap, state):
        return combine(
            state, jax.tree.map(lambda a: lax.dynamic_index_in_dim(a, lap, 0, False), gathered)
        )

    return lax.fori_loop(0, place, one, state)


def unit_rows(matrix):
    return matrix * lax.rsqrt(jnp.sum(matrix * matrix, axis=-1, keepdims=True) + 1e-06)


def block_terms(query_block, key_block, value_block, beta_block, decay_block):
    key_dim = query_block.shape[-1]
    copies = value_block.shape[1] // query_block.shape[1]
    length = query_block.shape[0]
    query_unit = unit_rows(query_block.astype(jnp.float32)) * key_dim ** (-0.5)
    key_unit = unit_rows(key_block.astype(jnp.float32))
    query_heads = jnp.transpose(jnp.repeat(query_unit, copies, axis=1), (1, 0, 2))
    key_heads = jnp.transpose(jnp.repeat(key_unit, copies, axis=1), (1, 0, 2))
    value_heads = jnp.transpose(value_block.astype(jnp.float32), (1, 0, 2))
    beta_rows = jnp.transpose(beta_block)
    cumulative = jnp.cumsum(jnp.transpose(decay_block), axis=1)
    row_ids = lax.broadcasted_iota(jnp.int32, (length, length), 0)
    col_ids = lax.broadcasted_iota(jnp.int32, (length, length), 1)
    inclusive = row_ids >= col_ids
    strict = row_ids > col_ids
    spread = cumulative[:, :, None] - cumulative[:, None, :]
    fading = jnp.where(inclusive, jnp.exp(jnp.where(inclusive, spread, 0.0)), 0.0)
    key_key = jnp.einsum("hid,hjd->hij", key_heads, key_heads, precision=HIGHEST_PREC)
    query_key = jnp.einsum("hid,hjd->hij", query_heads, key_heads, precision=HIGHEST_PREC)
    unit_lower = jnp.where(strict, beta_rows[:, :, None] * fading * key_key, 0.0) + jnp.eye(
        length, dtype=jnp.float32
    )
    growth = jnp.exp(cumulative)
    right_cols = jnp.concatenate(
        [(beta_rows * growth)[:, :, None] * key_heads, beta_rows[:, :, None] * value_heads], axis=2
    )
    solved = lax.linalg.triangular_solve(
        unit_lower, right_cols, left_side=True, lower=True, unit_diagonal=True
    )
    weighted_keys = solved[:, :, :key_dim]
    base_values = solved[:, :, key_dim:]
    mixing = fading * query_key
    query_reach = growth[:, :, None] * query_heads - jnp.einsum(
        "hij,hjd->hid", mixing, weighted_keys, precision=HIGHEST_PREC
    )
    local_rows = jnp.einsum("hij,hjv->hiv", mixing, base_values, precision=HIGHEST_PREC)
    tail_fade = jnp.exp(cumulative[:, -1:] - cumulative)
    tail_keys = tail_fade[:, :, None] * key_heads
    carry_map = growth[:, -1][:, None, None] * jnp.eye(key_dim, dtype=jnp.float32) - jnp.einsum(
        "hcd,hce->hde", weighted_keys, tail_keys, precision=HIGHEST_PREC
    )
    offset = jnp.einsum("hcv,hcd->hvd", base_values, tail_keys, precision=HIGHEST_PREC)
    return (local_rows, query_reach, carry_map, offset)


def gated_norm(results, out_gate, norm_gain):
    norm_scale = lax.rsqrt(jnp.mean(results * results, axis=-1, keepdims=True) + 1e-06)
    gate_f32 = out_gate.astype(jnp.float32)
    return (results * norm_scale * norm_gain * jax.nn.silu(gate_f32)).astype(jnp.bfloat16)


def compose(earlier_pair, later_pair):
    joined_map = jnp.einsum("hde,hef->hdf", earlier_pair[0], later_pair[0], precision=HIGHEST_PREC)
    joined_offset = (
        jnp.einsum("hvd,hde->hve", earlier_pair[1], later_pair[0], precision=HIGHEST_PREC)
        + later_pair[1]
    )
    return (joined_map, joined_offset)


def identity_pair(head_count, key_dim, value_dim):
    identity_maps = jnp.broadcast_to(
        jnp.eye(key_dim, dtype=jnp.float32), (head_count, key_dim, key_dim)
    )
    zero_offsets = jnp.zeros((head_count, value_dim, key_dim), jnp.float32)
    return (identity_maps, zero_offsets)


def advance(carried, pieces):
    local_rows, query_reach, carry_map, offset = block_terms(*pieces)
    results = local_rows + jnp.einsum(
        "hcd,hvd->hcv", query_reach, carried[1], precision=HIGHEST_PREC
    )
    reach_rows = jnp.einsum("hcd,hed->hce", query_reach, carried[0], precision=HIGHEST_PREC)
    return (compose(carried, (carry_map, offset)), (results, reach_rows))


def in_blocks(array):
    return array.reshape((array.shape[0] // BLOCK, BLOCK) + array.shape[1:])


def run_slab(pieces, head_count, key_dim, value_dim):
    tok_rows = pieces[0].shape[0]
    blocked = tuple((in_blocks(piece) for piece in pieces))
    final_pair, (local_out, local_reach) = lax.scan(
        advance, identity_pair(head_count, key_dim, value_dim), blocked
    )
    local_out = jnp.transpose(local_out, (0, 2, 1, 3)).reshape((tok_rows, head_count, value_dim))
    local_reach = jnp.transpose(local_reach, (0, 2, 1, 3)).reshape((tok_rows, head_count, key_dim))
    return (final_pair, local_out, local_reach)


def body(queries, keys, values, beta, log_decay, out_gate, norm_gain):
    key_dim = queries.shape[2]
    head_count = values.shape[1]
    value_dim = values.shape[2]
    group_size = lax.axis_size("head")
    head_local = head_count // group_size
    moved_q, moved_k, moved_v, moved_gate = (
        lax.all_to_all(queries, "head", split_axis=1, concat_axis=0, tiled=True),
        lax.all_to_all(keys, "head", split_axis=1, concat_axis=0, tiled=True),
        lax.all_to_all(values, "head", split_axis=1, concat_axis=0, tiled=True),
        lax.all_to_all(out_gate, "head", split_axis=1, concat_axis=0, tiled=True),
    )
    moved_beta, moved_decay = (
        lax.all_to_all(beta, "head", split_axis=1, concat_axis=0, tiled=True),
        lax.all_to_all(log_decay, "head", split_axis=1, concat_axis=0, tiled=True),
    )
    slab_pair, slab_out, slab_reach = run_slab(
        (moved_q, moved_k, moved_v, moved_beta, moved_decay), head_local, key_dim, value_dim
    )
    _, state_in = entering(slab_pair, "seq", compose, identity_pair(head_local, key_dim, value_dim))
    results = slab_out + jnp.einsum("thd,hvd->thv", slab_reach, state_in, precision=HIGHEST_PREC)
    return gated_norm(results, moved_gate, norm_gain)


def solution(mesh):
    return jax.shard_map(
        body,
        mesh=mesh,
        in_specs=(
            P(("seq", "head"), None, None),
            P(("seq", "head"), None, None),
            P(("seq", "head"), None, None),
            P(("seq", "head"), None),
            P(("seq", "head"), None),
            P(("seq", "head"), None, None),
            P(),
        ),
        out_specs=P("seq", "head", None),
        check_vma=False,
    )
```

profile of v0, /device:TPU:27, one launch (start us, length us, event | category | flops | bytes accessed | tf_op | source)
XLA Modules:
  0.0 337.7 jit_solution(5375670007343504209)
XLA Ops:
  6.5 6.4 %all_to_all.86 = f32[128,4,4]{0,2,1:T(4,128)S(1)} all-to-all(f32[128,4,4]{0,2,1:T(4,128)} %bitcast.214), channel_id=1, replica_groups=mesh['seq'=8,'head'=4] {'head'}, dimensions={1} | all-to-all | bytes 16384 | tf_op jit(solution)/shard_map/all_to_all | solution.py:135
  13.0 4.1 %all-to-all-start.1 = ((f32[128,4,4]{0,2,1:T(4,128)}), f32[128,4,4]{0,2,1:T(4,128)S(1)}, u32[]{:S(2)}, u32[]{:S(2)}) async-start(f32[128,4,4]{0,2,1:T(4,128)} %bitcast.215), calls=%async_computation.1 | async-start | bytes 16384 | tf_op jit(solution)/shard_map/all_to_all | solution.py:134
  17.1 2.0 copy.57
  19.5 4.6 %all-to-all-start.3 = ((bf16[128,16,128]{2,0,1:T(8,128)(2,1)}), bf16[128,16,128]{2,0,1:T(8,128)(2,1)S(1)}, u32[]{:S(2)}, u32[]{:S(2)}) async-start(bf16[128,16,128]{2,0,1:T(8,128)(2,1)} %copy.57), calls=%async_computation.3 | async-start | bytes 1048576 | tf_op jit(solution)/shard_map/all_to_all | solution.py:130
  25.0 4.2 %all-to-all-done.3 = bf16[128,16,128]{2,0,1:T(8,128)(2,1)S(1)} async-done(((bf16[128,16,128]{2,0,1:T(8,128)(2,1)}), bf16[128,16,128]{2,0,1:T(8,128)(2,1)S(1)}, u32[]{:S(2)}, u32[]{:S(2)}) %all-to-all-start.3) | async-done | bytes 524320 | tf_op jit(solution)/shard_map/all_to_all | solution.py:130
  29.3 3.8 %all-to-all-start.4 = ((bf16[128,16,128]{2,0,1:T(8,128)(2,1)}), bf16[128,16,128]{2,0,1:T(8,128)(2,1)S(1)}, u32[]{:S(2)}, u32[]{:S(2)}) async-start(bf16[128,16,128]{2,0,1:T(8,128)(2,1)} %copy.58), calls=%async_computation.4 | async-start | bytes 1048576 | tf_op jit(solution)/shard_map/all_to_all | solution.py:128
  34.0 4.2 %all-to-all-done.4 = bf16[128,16,128]{2,0,1:T(8,128)(2,1)S(1)} async-done(((bf16[128,16,128]{2,0,1:T(8,128)(2,1)}), bf16[128,16,128]{2,0,1:T(8,128)(2,1)S(1)}, u32[]{:S(2)}, u32[]{:S(2)}) %all-to-all-start.4) | async-done | bytes 524320 | tf_op jit(solution)/shard_map/all_to_all | solution.py:128
  38.2 3.7 %all-to-all-start.2 = ((bf16[128,16,128]{2,0,1:T(8,128)(2,1)}), bf16[128,16,128]{2,0,1:T(8,128)(2,1)S(1)}, u32[]{:S(2)}, u32[]{:S(2)}) async-start(bf16[128,16,128]{2,0,1:T(8,128)(2,1)} %copy.56), calls=%async_computation.2 | async-start | bytes 1048576 | tf_op jit(solution)/shard_map/all_to_all | solution.py:129
  42.0 5.1 %all-to-all-done.2 = bf16[128,16,128]{2,0,1:T(8,128)(2,1)S(1)} async-done(((bf16[128,16,128]{2,0,1:T(8,128)(2,1)}), bf16[128,16,128]{2,0,1:T(8,128)(2,1)S(1)}, u32[]{:S(2)}, u32[]{:S(2)}) %all-to-all-start.2) | async-done | bytes 524320 | tf_op jit(solution)/shard_map/all_to_all | solution.py:129
  47.1 195.4 %while.30 = (s32[]{:T(128)}, f32[4,128,128]{1,2,0:T(8,128)S(1)}, f32[4,128,128]{1,2,0:T(8,128)S(1)}, f32[4,4,128,128]{3,2,1,0:T(8,128)}, f32[4,4,128,128]{3,2,0,...) while((s32[]{:T(128)}, f32[4,128,128]{1,2,0:T(8,128)S(1)}, ...), condition=%wide.region_4.5_spmd.clone, body=%wide.region_0.4_spmd.clone.sunk | while | flops 1211417216 | bytes 10999552 | solution.py:113
  48.9 39.3 %custom-call.8 = f32[4,1,128,128]{2,3,1,0:T(8,128)S(1)} custom-call(f32[4,1,128,128]{3,2,1,0:T(8,128)S(1)} %fusion.144), custom_call_target="InvertDiagBlocksLowerTriangular" | custom-call | tf_op jit(solution)/shard_map/while/body/eval_jaxpr/triangular_solve | solution.py:55
  97.8 39.3 %custom-call.8 = f32[4,1,128,128]{2,3,1,0:T(8,128)S(1)} custom-call(f32[4,1,128,128]{3,2,1,0:T(8,128)S(1)} %fusion.144), custom_call_target="InvertDiagBlocksLowerTriangular" | custom-call | tf_op jit(solution)/shard_map/while/body/eval_jaxpr/triangular_solve | solution.py:55
  146.6 39.3 %custom-call.8 = f32[4,1,128,128]{2,3,1,0:T(8,128)S(1)} custom-call(f32[4,1,128,128]{3,2,1,0:T(8,128)S(1)} %fusion.144), custom_call_target="InvertDiagBlocksLowerTriangular" | custom-call | tf_op jit(solution)/shard_map/while/body/eval_jaxpr/triangular_solve | solution.py:55
  195.5 39.3 %custom-call.8 = f32[4,1,128,128]{2,3,1,0:T(8,128)S(1)} custom-call(f32[4,1,128,128]{3,2,1,0:T(8,128)S(1)} %fusion.144), custom_call_target="InvertDiagBlocksLowerTriangular" | custom-call | tf_op jit(solution)/shard_map/while/body/eval_jaxpr/triangular_solve | solution.py:55
  244.4 2.1 copy.66
  246.4 3.8 %all-to-all-start.5 = ((bf16[128,16,128]{2,0,1:T(8,128)(2,1)}), bf16[128,16,128]{2,0,1:T(8,128)(2,1)S(1)}, u32[]{:S(2)}, u32[]{:S(2)}) async-start(bf16[128,16,128]{2,0,1:T(8,128)(2,1)} %copy.66), calls=%async_computation.5 | async-start | bytes 1048576 | tf_op jit(solution)/shard_map/all_to_all | solution.py:131
  251.0 4.3 %all-to-all-done.5 = bf16[128,16,128]{2,0,1:T(8,128)(2,1)S(1)} async-done(((bf16[128,16,128]{2,0,1:T(8,128)(2,1)}), bf16[128,16,128]{2,0,1:T(8,128)(2,1)S(1)}, u32[]{:S(2)}, u32[]{:S(2)}) %all-to-all-start.5) | async-done | bytes 524320 | tf_op jit(solution)/shard_map/all_to_all | solution.py:131
  257.9 19.7 %all-gather.5.cloned.1.call-done = f32[32,128,128]{2,1,0:T(8,128)} async-done(((f32[4,128,128]{2,1,0:T(8,128)}), f32[32,128,128]{2,1,0:T(8,128)}) %all-gather.5.cloned.1.call-update) | async-done | bytes 2097168 | tf_op jit(solution)/shard_map/all_gather | solution.py:14
  277.6 30.2 %all-gather.7.cloned.1.call-done = f32[32,128,128]{2,1,0:T(8,128)} async-done(((f32[4,128,128]{2,1,0:T(8,128)}), f32[32,128,128]{2,1,0:T(8,128)}) %all-gather.7.cloned.1.call-update) | async-done | bytes 2097168 | tf_op jit(solution)/shard_map/all_gather | solution.py:14
  307.8 19.1 %while.29 = (s32[]{:T(128)}, f32[4,128,128]{1,2,0:T(8,128)S(1)}, s32[]{:T(128)}, f32[8,4,128,128]{3,2,1,0:T(8,128)}, f32[8,4,128,128]{3,2,1,0:T(8,128)}, /*index=5*/s32[]{:T(128)}, s32[]{:T(128)}, s32[]{:T(128)}) while((s32[]{:T(128)}, f32[4,128,128]{1,2,0:T(8,128)S(1)}, s32[]{:T(128)}, f32[8,4,128,128]{3,2,1,0:T(8,128)}, ...), condition=%wide.region_6.7_spmd, body=%wide.region_5.6_spmd.sunk | while | flops 100728832 | bytes 2621567 | solution.py:22
  309.0 1.6 fusion.118
  314.4 1.6 fusion.118
  322.6 1.6 fusion.118
  327.0 2.4 multiply_reduce_fusion
  (161 shorter events, 60.5 us)
Async XLA Ops:
  6.5 17.6 %copy-start.2 = (bf16[128,16,128]{2,1,0:T(8,128)(2,1)S(1)}, bf16[128,16,128]{2,1,0:T(8,128)(2,1)}, u32[]{:S(2)}) copy-start(bf16[128,16,128]{2,1,0:T(8,128)(2,1)} %param.11) | copy-start | bytes 1572868
  13.0 6.5 %all-to-all-start.1 = ((f32[128,4,4]{0,2,1:T(4,128)}), f32[128,4,4]{0,2,1:T(4,128)S(1)}, u32[]{:S(2)}, u32[]{:S(2)}) async-start(f32[128,4,4]{0,2,1:T(4,128)} %bitcast.215), calls=%async_computation.1 | async-start | bytes 16384 | tf_op jit(solution)/shard_map/all_to_all | solution.py:134
  17.1 15.9 %copy-start.3 = (bf16[128,16,128]{2,1,0:T(8,128)(2,1)S(1)}, bf16[128,16,128]{2,1,0:T(8,128)(2,1)}, u32[]{:S(2)}) copy-start(bf16[128,16,128]{2,1,0:T(8,128)(2,1)} %param.12) | copy-start | bytes 1572868
  19.5 9.8 %all-to-all-start.3 = ((bf16[128,16,128]{2,0,1:T(8,128)(2,1)}), bf16[128,16,128]{2,0,1:T(8,128)(2,1)S(1)}, u32[]{:S(2)}, u32[]{:S(2)}) async-start(bf16[128,16,128]{2,0,1:T(8,128)(2,1)} %copy.57), calls=%async_computation.3 | async-start | bytes 1048576 | tf_op jit(solution)/shard_map/all_to_all | solution.py:130
  29.3 8.9 %all-to-all-start.4 = ((bf16[128,16,128]{2,0,1:T(8,128)(2,1)}), bf16[128,16,128]{2,0,1:T(8,128)(2,1)S(1)}, u32[]{:S(2)}, u32[]{:S(2)}) async-start(bf16[128,16,128]{2,0,1:T(8,128)(2,1)} %copy.58), calls=%async_computation.4 | async-start | bytes 1048576 | tf_op jit(solution)/shard_map/all_to_all | solution.py:128
  38.2 8.9 %all-to-all-start.2 = ((bf16[128,16,128]{2,0,1:T(8,128)(2,1)}), bf16[128,16,128]{2,0,1:T(8,128)(2,1)S(1)}, u32[]{:S(2)}, u32[]{:S(2)}) async-start(bf16[128,16,128]{2,0,1:T(8,128)(2,1)} %copy.56), calls=%async_computation.2 | async-start | bytes 1048576 | tf_op jit(solution)/shard_map/all_to_all | solution.py:129
  41.9 235.7 %all-gather.5.cloned.1.call-start = ((), (), s32[]{:S(2)}) async-start(), calls=%async_computation.6 | async-start | bytes 2359296 | tf_op jit(solution)/shard_map/all_gather | solution.py:14
  243.4 64.4 %all-gather.7.cloned.1.call-start = ((), (), s32[]{:S(2)}) async-start(), calls=%async_computation.7 | async-start | bytes 2359296 | tf_op jit(solution)/shard_map/all_gather | solution.py:14
  244.3 5.9 %copy-start.1 = (f32[4,4,128,128]{3,2,1,0:T(8,128)S(1)}, f32[4,4,128,128]{3,2,1,0:T(8,128)}, u32[]{:S(2)}) copy-start(f32[4,4,128,128]{3,2,1,0:T(8,128)} %get-tuple-element.104) | copy-start | bytes 3145732
  246.4 8.9 %all-to-all-start.5 = ((bf16[128,16,128]{2,0,1:T(8,128)(2,1)}), bf16[128,16,128]{2,0,1:T(8,128)(2,1)S(1)}, u32[]{:S(2)}, u32[]{:S(2)}) async-start(bf16[128,16,128]{2,0,1:T(8,128)(2,1)} %copy.66), calls=%async_computation.5 | async-start | bytes 1048576 | tf_op jit(solution)/shard_map/all_to_all | solution.py:131
  255.3 0.8 copy-start
  326.9 2.4 copy-start.4
Sparse Core Ops, SparseCore 0:
  243.6 34.0 all-gather.4
  279.2 28.5 all-gather.6
where the time goes:
time: 339 us; the launch traced here: 338 us
  other arithmetic  162 us (48%)
  waiting for transfers between devices  68.2 us (20%)
  matrix products  44.9 us (13%)
  local copies, waits for them, and re-layouts  21.6 us (6%)
  starting transfers between devices  20.1 us (6%)
  between operations  13.5 us (4%)
  blocking collectives  6.43 us (2%)
    another operation x16, other arithmetic, block_terms(): lax.linalg.triangular_solve(unit_lower, right_cols, left_side=True, lower...  158 us
    all_gather x2, waiting for transfers between devices, entering(): gathered = jax.tree.map(lambda a: lax.all_gather(a, axis), part)  49.9 us
    dot_general x11, matrix products, compose(): jnp.einsum('hvd,hde->hve', earlier_pair[1], later_pair[0], precision=HIGH...  13.3 us
    dynamic_slice x14, local copies, waits for them, and re-layouts, one(): lax.dynamic_index_in_dim(a, lap, 0, False)  7.71 us
  transfers between devices with their start and end apart: 7, of which 7 were waited for; matrix products, arithmetic and copies ran while one was open for 3% of the time, Pallas kernels for 0%

commit v1 on v0

v1 whole, which is shorter than its diff:
```python
import functools

import jax
import jax.numpy as jnp
from jax import lax
from jax.experimental import pallas as pl
from jax.experimental.pallas import tpu as pltpu
from jax.sharding import PartitionSpec as P

MESH = pl.DeviceIdType.MESH
F32 = jnp.float32
BF16 = jnp.bfloat16
NN = (((1,), (0,)), ((), ()))
NT = (((1,), (1,)), ((), ()))
TN = (((0,), (0,)), ((), ()))


def dot(a, b, dims=NN):
    return lax.dot_general(a, b, dims, preferred_element_type=F32)


def split(x):
    hi = x.astype(BF16)
    return hi, (x - hi.astype(F32)).astype(BF16)


def cat(parts, axis):
    return jnp.concatenate(parts, axis=axis)


def lhs_pair(x):
    return cat(split(x), 1)


def rhs_square(x):
    both = cat(split(x), 1)
    return cat((both, both), 0)


def mm(lhs, rhs):
    wide = dot(lhs, rhs)
    half = wide.shape[1] // 2
    return wide[:, :half] + wide[:, half:]


def mm_nt(a, b):
    a_hi, a_lo = split(a)
    b_hi, b_lo = split(b)
    return dot(cat((a_hi, a_lo), 1), cat((b_hi, b_hi), 1), NT) + dot(a_hi, b_lo, NT)


def kernel(
    n, steps, heads, bd_hbm, k_hbm, v_hbm, q_hbm, g_hbm, gain_ref, out_ref,
    bd, kb, vb, qb, gb, fade, grow, wu, pairs, prefix, slab, local, reach,
    state_in, state_out, send_sem, recv_sem, chain_send, chain_recv,
):
    me = lax.axis_index("head")
    place = lax.axis_index("seq")
    after = lax.rem(place + 1, steps)
    before = lax.rem(place + steps - 1, steps)
    length, depth = kb.shape[2], kb.shape[3]

    barrier = pltpu.get_barrier_semaphore()
    for d in range(1, n):
        pl.semaphore_signal(
            barrier, inc=1, device_id={"head": lax.rem(me + d, n)}, device_id_type=MESH
        )
    pl.semaphore_signal(barrier, inc=1, device_id={"seq": before}, device_id_type=MESH)
    pl.semaphore_wait(barrier, n)

    sources = (bd_hbm, k_hbm, v_hbm, q_hbm, g_hbm)
    targets = (bd, kb, vb, qb, gb)

    def remote(t, d):
        peer = lax.rem(me + d, n)
        return pltpu.make_async_remote_copy(
            src_ref=sources[t].at[peer],
            dst_ref=targets[t].at[me],
            send_sem=send_sem.at[t, d],
            recv_sem=recv_sem.at[t, n - d],
            device_id={"head": peer},
            device_id_type=MESH,
        )

    def own(t):
        return pltpu.make_async_copy(sources[t].at[me], targets[t].at[me], recv_sem.at[t, 0])

    def arrived(t, d):
        came = lax.rem(me + d, n)
        return pltpu.make_async_remote_copy(
            src_ref=sources[t].at[came],
            dst_ref=targets[t].at[came],
            send_sem=send_sem.at[t, d],
            recv_sem=recv_sem.at[t, d],
            device_id={"head": came},
            device_id_type=MESH,
        )

    for t in range(5):
        own(t).start()
        for d in range(1, n):
            remote(t, d).start()

    def wait_for(t, d):
        @pl.when(d == 0)
        def _():
            own(t).wait()

        @pl.when(d > 0)
        def _():
            arrived(t, d).wait_recv()

    rows = lax.broadcasted_iota(jnp.int32, (length, length), 0)
    cols = lax.broadcasted_iota(jnp.int32, (length, length), 1)
    eye = rows == cols
    inclusive = rows >= cols
    strict = rows > cols
    one = jnp.where(eye, 1.0, 0.0)

    def block_step(d, carry):
        s = lax.rem(me + d, n)
        wait_for(0, d)
        wait_for(1, d)
        keys, lower, scales = [], [], []
        for h in range(heads):
            key = kb[s, h]
            beta_row = bd[s, pl.ds(h, 1), :]
            decay_row = bd[s, pl.ds(heads + h, 1), :]
            cum_col = jnp.sum(jnp.where(inclusive, decay_row, 0.0), axis=1, keepdims=True)
            cum_row = jnp.sum(jnp.where(eye, cum_col, 0.0), axis=0, keepdims=True)
            beta_col = jnp.sum(jnp.where(eye, beta_row, 0.0), axis=1, keepdims=True)
            kk = dot(key, key, NT)
            on_diag = jnp.where(eye, kk, 0.0)
            norm_row = lax.rsqrt(jnp.sum(on_diag, axis=0, keepdims=True) + 1e-06)
            norm_col = lax.rsqrt(jnp.sum(on_diag, axis=1, keepdims=True) + 1e-06)
            fading = jnp.where(
                inclusive, jnp.exp(jnp.where(inclusive, cum_col - cum_row, 0.0)), 0.0
            ) * norm_row
            fade[s, h] = fading
            grow_col = jnp.exp(cum_col)
            grow[s, h] = jnp.broadcast_to(grow_col, (length, depth))
            lower.append(jnp.where(strict, (beta_col * norm_col) * fading * kk, 0.0))
            last = cum_row[:, length - 1 :]
            tail = jnp.exp(last - cum_col) * norm_col
            scales.append((beta_row, beta_row * norm_row * jnp.exp(cum_row), tail, jnp.exp(last)))
            keys.append(key)
        inverse = [one - jnp.where((rows // 2) == (cols // 2), low, 0.0) for low in lower]
        size = 2
        while size < length:
            pick = ((rows // (2 * size)) == (cols // (2 * size))) & (
                (rows // size) != (cols // size)
            )
            crosses = [lhs_pair(jnp.where(pick, low, 0.0)) for low in lower]
            halves = [split(x) for x in inverse]
            lefts = [cat(pair, 1) for pair in halves]
            rights = [cat((left, left), 0) for left in lefts]
            middles = [mm(c, r) for c, r in zip(crosses, rights)]
            products = [mm(l, rhs_square(m)) for l, m in zip(lefts, middles)]
            inverse = [x - p for x, p in zip(inverse, products)]
            size *= 2
        wait_for(2, d)
        for h in range(heads):
            beta_row, key_row, tail, last = scales[h]
            key = keys[h]
            value = vb[s, h]
            w = dot(lhs_pair(inverse[h] * key_row), cat((key, key), 0))
            u = dot(lhs_pair(inverse[h] * beta_row), cat((value, value), 0))
            both = cat((w, u), 1)
            wu[s, h] = both
            hi, lo = split(both * tail)
            moved = dot(cat((hi, lo), 0), cat((key, key), 0), TN)
            pairs[s, h, :depth] = last * one - moved[:depth]
            pairs[s, h, depth:] = moved[depth:]
        return carry

    lax.fori_loop(0, n, block_step, 0)

    for h in range(heads):
        slab[h] = pairs[0, h]

    def compose(s, carry):
        for h in range(heads):
            now = slab[h]
            prefix[s, h] = now
            step = pairs[s, h]
            joined = mm(lhs_pair(now), rhs_square(step[:depth]))
            slab[h, :depth] = joined[:depth]
            slab[h, depth:] = joined[depth:] + step[depth:]
        return carry

    lax.fori_loop(1, n, compose, 0)

    def local_step(d, carry):
        s = lax.rem(me + d, n)
        wait_for(3, d)
        for h in range(heads):
            query = qb[s, h]
            qf = query.astype(F32)
            norm = lax.rsqrt(jnp.sum(qf * qf, axis=1, keepdims=True) + 1e-06) * depth ** (-0.5)
            mixing = dot(query, kb[s, h], NT) * norm * fade[s, h]
            m_hi, m_lo = split(mixing)
            wu_hi, wu_lo = split(wu[s, h])
            mixed = dot(cat((m_hi, m_lo), 1), cat((wu_hi, wu_hi), 0)) + dot(m_hi, wu_lo)
            near = grow[s, h] * (qf * norm) - mixed[:, :depth]
            reach[s, h] = near
            local[s, h] = mixed[:, depth:]

        @pl.when(s > 0)
        def _():
            for h in range(heads):
                joined = mm_nt(reach[s, h], prefix[s, h])
                reach[s, h] = joined[:, :depth]
                local[s, h] += joined[:, depth:]

        return carry

    @pl.when(place >= steps // 2)
    def _():
        lax.fori_loop(0, n, local_step, 0)

    def onward(h):
        return pltpu.make_async_remote_copy(
            src_ref=state_out.at[h],
            dst_ref=state_in.at[h],
            send_sem=chain_send.at[h],
            recv_sem=chain_recv.at[h],
            device_id={"seq": after},
            device_id_type=MESH,
        )

    @pl.when(place == 0)
    def _():
        for h in range(heads):
            state_in[h] = jnp.zeros((depth, depth), F32)
            state_out[h] = slab[h, depth:]
            onward(h).start()

    @pl.when(place > 0)
    def _():
        for h in range(heads):
            right = rhs_square(slab[h, :depth])
            onward(h).wait_recv()
            state_out[h] = mm(lhs_pair(state_in[h]), right) + slab[h, depth:]

            @pl.when(place < steps - 1)
            def _():
                onward(h).start()

    @pl.when(place < steps // 2)
    def _():
        lax.fori_loop(0, n, local_step, 0)

    gain = gain_ref[...]

    def finish(d, carry):
        s = lax.rem(me + d, n)
        wait_for(4, d)
        for h in range(heads):
            result = local[s, h] + mm_nt(reach[s, h], state_in[h])
            scale = lax.rsqrt(jnp.mean(result * result, axis=1, keepdims=True) + 1e-06)
            gate = gb[s, h].astype(F32)
            gated = result * scale * gain * (gate / (1.0 + jnp.exp(-gate)))
            out_ref[h, pl.ds(pl.multiple_of(s * length, length), length), :] = gated.astype(BF16)
        return carry

    lax.fori_loop(0, n, finish, 0)

    for t in range(5):
        for d in range(1, n):
            remote(t, d).wait_send()

    @pl.when(place < steps - 1)
    def _():
        for h in range(heads):
            onward(h).wait_send()


def body(n, steps, queries, keys, values, beta, log_decay, out_gate, norm_gain):
    length, all_heads, depth = keys.shape
    heads = all_heads // n

    def regroup(x):
        return jnp.transpose(x.reshape(length, n, heads, depth), (1, 2, 0, 3))

    def rows_of(x):
        return jnp.transpose(x).reshape(n, heads, length)

    padded = -(-2 * heads // 8) * 8
    bd = jnp.concatenate(
        [rows_of(beta), rows_of(log_decay), jnp.zeros((n, padded - 2 * heads, length), F32)], axis=1
    )
    big = (n, heads, length, depth)
    any_spec = pl.BlockSpec(memory_space=pl.ANY)
    vmem = pl.BlockSpec(memory_space=pltpu.VMEM)
    out = pl.pallas_call(
        functools.partial(kernel, n, steps, heads),
        out_shape=jax.ShapeDtypeStruct((heads, n * length, depth), BF16),
        in_specs=[any_spec] * 5 + [vmem],
        out_specs=vmem,
        scratch_shapes=[
            pltpu.VMEM((n, padded, length), F32),
            pltpu.VMEM(big, BF16),
            pltpu.VMEM(big, BF16),
            pltpu.VMEM(big, BF16),
            pltpu.VMEM(big, BF16),
            pltpu.VMEM((n, heads, length, length), F32),
            pltpu.VMEM(big, F32),
            pltpu.VMEM((n, heads, length, 2 * depth), F32),
            pltpu.VMEM((n, heads, 2 * depth, depth), F32),
            pltpu.VMEM((n, heads, 2 * depth, depth), F32),
            pltpu.VMEM((heads, 2 * depth, depth), F32),
            pltpu.VMEM(big, F32),
            pltpu.VMEM(big, F32),
            pltpu.VMEM((heads, depth, depth), F32),
            pltpu.VMEM((heads, depth, depth), F32),
            pltpu.SemaphoreType.DMA((5, n)),
            pltpu.SemaphoreType.DMA((5, n)),
            pltpu.SemaphoreType.DMA((heads,)),
            pltpu.SemaphoreType.DMA((heads,)),
        ],
        compiler_params=pltpu.CompilerParams(
            collective_id=0, has_side_effects=True, vmem_limit_bytes=48 * 1024 * 1024
        ),
    )(bd, regroup(keys), regroup(values), regroup(queries), regroup(out_gate), norm_gain[None, :])
    return jnp.transpose(out, (1, 0, 2))


def solution(mesh):
    return jax.shard_map(
        functools.partial(body, mesh.shape["head"], mesh.shape["seq"]),
        mesh=mesh,
        in_specs=(
            P(("seq", "head"), None, None),
            P(("seq", "head"), None, None),
            P(("seq", "head"), None, None),
            P(("seq", "head"), None),
            P(("seq", "head"), None),
            P(("seq", "head"), None, None),
            P(),
        ),
        out_specs=P("seq", "head", None),
        check_vma=False,
    )
```

time: 339 us -> 47 us (0.14)
  other arithmetic: 162 us -> 0.72 us
  waiting for transfers between devices: 68.2 us -> 0 us
  matrix products: 44.9 us -> 0 us
  Pallas kernels: 0 us -> 40.6 us
  starting transfers between devices: 20.1 us -> 0 us
  local copies, waits for them, and re-layouts: 21.6 us -> 5.3 us
  between operations: 13.5 us -> 0.05 us
  blocking collectives: 6.43 us -> 0 us
    another operation x22 -> x0, other arithmetic: 159 us -> none  [the longest x16 158 us: block_terms(): lax.linalg.triangular_solve(unit_lower, right_cols, left_side=True, lower...]
    all_gather x2 -> x0, waiting for transfers between devices: 49.9 us -> none  [entering(): gathered = jax.tree.map(lambda a: lax.all_gather(a, axis), part)]
    dot_general x48 -> x0, matrix products: 42.4 us -> none  [the longest x11 13.3 us: compose(): jnp.einsum('hvd,hde->hve', earlier_pair[1], later_pair[0], precision=HIGH...]
    pallas_call x0 -> x1, Pallas kernels: none -> 40.6 us  [body(): pl.pallas_call(functools.partial(kernel, n, steps, heads), out_shape=jax....]
    all_to_all x5 -> x0, starting transfers between devices: 20 us -> none  [the longest x1 4.6 us: body(): lax.all_to_all(values, 'head', split_axis=1, concat_axis=0, tiled=True)]
    all_to_all x5 -> x0, waiting for transfers between devices: 18.3 us -> none  [the longest x1 5.14 us: body(): lax.all_to_all(keys, 'head', split_axis=1, concat_axis=0, tiled=True)]
    dynamic_slice x14 -> x0, local copies, waits for them, and re-layouts: 7.71 us -> none  [one(): lax.dynamic_index_in_dim(a, lap, 0, False)]
    all_to_all x1 -> x0, blocking collectives: 6.43 us -> none  [body(): lax.all_to_all(log_decay, 'head', split_axis=1, concat_axis=0, tiled=True)]
  transfers between devices with their start and end apart: 7 -> 0, of which waited for: 7 -> 0; matrix products, arithmetic and copies ran while one was open for 3% -> 0% of each run, Pallas kernels for 0% -> 0%
where the time goes in v1:
time: 47 us; the launch traced here: 46.7 us
  Pallas kernels  40.6 us (86%)
  local copies, waits for them, and re-layouts  5.3 us (11%)
  other arithmetic  0.72 us (2%)
    pallas_call x1, Pallas kernels, body(): pl.pallas_call(functools.partial(kernel, n, steps, heads), out_shape=jax....  40.6 us
    unnamed x12, local copies, waits for them, and re-layouts  4.1 us
    transpose x1, local copies, waits for them, and re-layouts, body(): return jnp.transpose(out, (1, 0, 2))  1.2 us

profile of v1, /device:TPU:27, one launch (start us, length us, event | category | flops | bytes accessed | tf_op | source)
XLA Modules:
  0.0 46.7 jit_solution(12752123343726885801)
XLA Ops:
  0.0 0.7 %pad_maximum_fusion.bd_hbm = f32[4,8,128]{2,1,0:T(8,128)S(1)} fusion(f32[4,4,128]{2,1,0:T(4,128)} %bitcast.26, f32[4,4,128]{2,1,0:T(4,128)} %bitcast.27), kind=kLoop, calls=%fused_computation | loop fusion | flops 4096 | bytes 32768 | tf_op jit(solution)/shard_map/concatenate | solution.py:289
  0.7 0.0 copy-start.1
  0.7 1.2 %copy.10 = bf16[128,16,128]{2,0,1:T(8,128)(2,1)S(1)} copy(bf16[128,16,128]{2,1,0:T(8,128)(2,1)} %param.7) | data formatting | bytes 1048576 | tf_op args[0]
  2.0 0.0 copy-done.1
  2.0 0.0 copy-start.2
  2.0 0.1 copy.8
  2.1 0.9 %copy-done.2 = bf16[128,16,128]{2,1,0:T(8,128)(2,1)S(1)} copy-done((bf16[128,16,128]{2,1,0:T(8,128)(2,1)S(1)}, bf16[128,16,128]{2,1,0:T(8,128)(2,1)}, u32[]{:S(2)}) %copy-start.2) | copy-done | bytes 524312
  3.0 0.0 copy-start.3
  3.0 0.1 copy.9
  3.2 0.9 %copy-done.3 = bf16[128,16,128]{2,1,0:T(8,128)(2,1)S(1)} copy-done((bf16[128,16,128]{2,1,0:T(8,128)(2,1)S(1)}, bf16[128,16,128]{2,1,0:T(8,128)(2,1)}, u32[]{:S(2)}) %copy-start.3) | copy-done | bytes 524312
  4.1 0.1 copy.11
  4.2 0.0 copy-start
  4.2 0.6 %copy-done = f32[128]{0:T(128)S(1)} copy-done((f32[128]{0:T(128)S(1)}, f32[128]{0:T(128)}, u32[]{:S(2)}) %copy-start) | copy-done | bytes 536
  4.9 40.6 %shard_map.73 = bf16[4,512,128]{2,1,0:T(8,128)(2,1)S(1)} custom-call(f32[4,8,128]{2,1,0:T(8,128)S(1)} %pad_maximum_fusion.bd_hbm, bf16[4,4,128,128]{3,2,1,0:T(8,128)(2,1)S(1)} %bitcast.22, bf16[4,4,128,128]{3,2,1,0:T(8,128)(2,1)S(1)} %bitcast.23, bf16[4,4,128,128]{3,2,1,0:T(8,128)(2,1)S(1)} %bitcast.21, bf16[4,4,128,128]{3,2,1,0:T(8,128)(2,1)S(1)} %bitcast.24, ...), custom_call_target="tpu_custom_call" | custom-call | tf_op jit(solution)/shard_map/pallas_call | solution.py:295
  45.5 1.2 %copy.12 = bf16[512,4,128]{2,1,0:T(4,128)(2,1)} copy(bf16[512,4,128]{2,0,1:T(8,128)(2,1)S(1)} %bitcast.20) | data formatting | bytes 1048576 | tf_op jit(solution)/shard_map/transpose | solution.py:325
Async XLA Ops:
  0.7 1.2 %copy-start.1 = (bf16[128,16,128]{2,1,0:T(8,128)(2,1)S(1)}, bf16[128,16,128]{2,1,0:T(8,128)(2,1)}, u32[]{:S(2)}) copy-start(bf16[128,16,128]{2,1,0:T(8,128)(2,1)} %param.8) | copy-start | bytes 1572868
  2.0 1.0 %copy-start.2 = (bf16[128,16,128]{2,1,0:T(8,128)(2,1)S(1)}, bf16[128,16,128]{2,1,0:T(8,128)(2,1)}, u32[]{:S(2)}) copy-start(bf16[128,16,128]{2,1,0:T(8,128)(2,1)} %param.9) | copy-start | bytes 1572868
  3.0 1.0 %copy-start.3 = (bf16[128,16,128]{2,1,0:T(8,128)(2,1)S(1)}, bf16[128,16,128]{2,1,0:T(8,128)(2,1)}, u32[]{:S(2)}) copy-start(bf16[128,16,128]{2,1,0:T(8,128)(2,1)} %param.12) | copy-start | bytes 1572868
  4.2 0.7 %copy-start = (f32[128]{0:T(128)S(1)}, f32[128]{0:T(128)}, u32[]{:S(2)}) copy-start(f32[128]{0:T(128)} %param.13) | copy-start | bytes 1540

commit v2 on v1

v2 whole, which is shorter than its diff:
```python
import functools

import jax
import jax.numpy as jnp
from jax import lax
from jax.experimental import pallas as pl
from jax.experimental.pallas import tpu as pltpu
from jax.sharding import PartitionSpec as P

MESH = pl.DeviceIdType.MESH
F32 = jnp.float32
BF16 = jnp.bfloat16
NN = (((1,), (0,)), ((), ()))
NT = (((1,), (1,)), ((), ()))
TN = (((0,), (0,)), ((), ()))


def dot(a, b, dims=NN):
    return lax.dot_general(a, b, dims, preferred_element_type=F32)


def split(x):
    hi = x.astype(BF16)
    return hi, (x - hi.astype(F32)).astype(BF16)


def cat(parts, axis):
    return jnp.concatenate(parts, axis=axis)


def lhs_pair(x):
    return cat(split(x), 1)


def rhs_square(x):
    both = cat(split(x), 1)
    return cat((both, both), 0)


def mm(lhs, rhs):
    wide = dot(lhs, rhs)
    half = wide.shape[1] // 2
    return wide[:, :half] + wide[:, half:]


def mm_nt(a, b):
    a_hi, a_lo = split(a)
    b_hi, b_lo = split(b)
    return dot(cat((a_hi, a_lo), 1), cat((b_hi, b_hi), 1), NT) + dot(a_hi, b_lo, NT)


def partner(me, d, n):
    if n & (n - 1):
        return lax.rem(2 * n + d - me, n)
    found, bit = 0, 1
    while bit < n:
        found += lax.rem(me // bit + d // bit, 2) * bit
        bit *= 2
    return found


def kernel(
    n, steps, heads, beta_hbm, decay_hbm, k_hbm, v_hbm, q_hbm, g_hbm, gain_hbm, out_ref,
    betas, decays, kb, vb, qb, gb, gain_ref, fade, grow, tails, solved, wu, pairs, prefix, slab,
    local, reach, state_in, state_out, send_sem, recv_sem, chain_send, chain_recv, gain_sem,
):
    me = lax.axis_index("head")
    place = lax.axis_index("seq")
    after = lax.rem(place + 1, steps)
    before = lax.rem(place + steps - 1, steps)
    length, depth = kb.shape[1], kb.shape[3]

    barrier = pltpu.get_barrier_semaphore()
    for d in range(1, n):
        pl.semaphore_signal(
            barrier, inc=1, device_id={"head": partner(me, d, n)}, device_id_type=MESH
        )
    pl.semaphore_signal(barrier, inc=1, device_id={"seq": before}, device_id_type=MESH)
    pl.semaphore_wait(barrier, n)

    sources = (beta_hbm, decay_hbm, k_hbm, v_hbm, q_hbm, g_hbm)
    targets = (betas, decays, kb, vb, qb, gb)
    kinds = len(sources)

    def part(t, peer):
        return sources[t].at[peer] if t < 2 else sources[t].at[:, peer]

    def remote(t, d):
        peer = partner(me, d, n)
        return pltpu.make_async_remote_copy(
            src_ref=part(t, peer),
            dst_ref=targets[t].at[me],
            send_sem=send_sem.at[t, d],
            recv_sem=recv_sem.at[t, d],
            device_id={"head": peer},
            device_id_type=MESH,
        )

    def own(t):
        return pltpu.make_async_copy(part(t, me), targets[t].at[me], recv_sem.at[t, 0])

    for t in range(kinds):
        own(t).start()
        for d in range(1, n):
            remote(t, d).start()
    pltpu.make_async_copy(gain_hbm, gain_ref, gain_sem).start()

    def wait_for(t, d):
        @pl.when(d == 0)
        def _():
            own(t).wait()

        @pl.when(d > 0)
        def _():
            remote(t, d).wait_recv()

    rows = lax.broadcasted_iota(jnp.int32, (length, length), 0)
    cols = lax.broadcasted_iota(jnp.int32, (length, length), 1)
    eye = rows == cols
    inclusive = rows >= cols
    strict = rows > cols
    one = jnp.where(eye, 1.0, 0.0)

    def heads_of(ref, s):
        return jnp.swapaxes(ref[s], 0, 1)

    group = 2 if n % 2 == 0 else 1

    def key_step(step, carry):
        lower, marks = [], []
        for j in range(group):
            d = step * group + j
            s = partner(me, d, n)
            for t in range(3):
                wait_for(t, d)
            keys = heads_of(kb, s)
            for h in range(heads):
                key = keys[h]
                beta_row = betas[s, pl.ds(h, 1), :]
                decay_row = decays[s, pl.ds(h, 1), :]
                cum_col = jnp.sum(jnp.where(inclusive, decay_row, 0.0), axis=1, keepdims=True)
                cum_row = jnp.sum(jnp.where(eye, cum_col, 0.0), axis=0, keepdims=True)
                beta_col = jnp.sum(jnp.where(eye, beta_row, 0.0), axis=1, keepdims=True)
                kk = dot(key, key, NT)
                on_diag = jnp.where(eye, kk, 0.0)
                norm_row = lax.rsqrt(jnp.sum(on_diag, axis=0, keepdims=True) + 1e-06)
                norm_col = lax.rsqrt(jnp.sum(on_diag, axis=1, keepdims=True) + 1e-06)
                fading = jnp.where(
                    inclusive, jnp.exp(jnp.where(inclusive, cum_col - cum_row, 0.0)), 0.0
                ) * norm_row
                fade[s, h] = fading
                grow[s, h] = jnp.broadcast_to(jnp.exp(cum_col), (length, depth))
                tail = jnp.exp(cum_row[:, length - 1 :] - cum_col) * norm_col
                tails[s, h] = jnp.broadcast_to(tail, (length, depth))
                lower.append(jnp.where(strict, (beta_col * norm_col) * fading * kk, 0.0))
                marks.append((s, h, key, beta_row, beta_row * norm_row * jnp.exp(cum_row)))
        inverse = [one - jnp.where((rows // 2) == (cols // 2), low, 0.0) for low in lower]
        size = 2
        while size < length:
            pick = ((rows // (2 * size)) == (cols // (2 * size))) & (
                (rows // size) != (cols // size)
            )
            crosses = [lhs_pair(jnp.where(pick, low, 0.0)) for low in lower]
            lefts = [lhs_pair(x) for x in inverse]
            middles = [mm(c, cat((left, left), 0)) for c, left in zip(crosses, lefts)]
            products = [mm(left, rhs_square(m)) for left, m in zip(lefts, middles)]
            inverse = [x - p for x, p in zip(inverse, products)]
            size *= 2
        for x, (s, h, key, beta_row, key_row) in zip(inverse, marks):
            wu[s, h, :, :depth] = dot(lhs_pair(x * key_row), cat((key, key), 0))
            solved[s, h] = lhs_pair(x * beta_row)
        return carry

    lax.fori_loop(0, n // group, key_step, 0)

    def value_step(d, carry):
        s = partner(me, d, n)
        wait_for(3, d)
        keys = heads_of(kb, s)
        values = heads_of(vb, s)
        for h in range(heads):
            key, value = keys[h], values[h]
            u = dot(solved[s, h], cat((value, value), 0))
            wu[s, h, :, depth:] = u
            tail = tails[s, h]
            hi, lo = split(cat((wu[s, h, :, :depth] * tail, u * tail), 1))
            moved = dot(cat((hi, lo), 0), cat((key, key), 0), TN)
            pairs[s, h, :depth] = grow[s, h, length - 1 :, :] * one - moved[:depth]
            pairs[s, h, depth:] = moved[depth:]
        return carry

    lax.fori_loop(0, n, value_step, 0)

    for h in range(heads):
        slab[h] = pairs[0, h]

    def compose(s, carry):
        for h in range(heads):
            now = slab[h]
            prefix[s, h] = now
            step = pairs[s, h]
            joined = mm(lhs_pair(now), rhs_square(step[:depth]))
            slab[h, :depth] = joined[:depth]
            slab[h, depth:] = joined[depth:] + step[depth:]
        return carry

    lax.fori_loop(1, n, compose, 0)

    def local_step(d, carry):
        s = partner(me, d, n)
        wait_for(4, d)
        keys = heads_of(kb, s)
        queries = heads_of(qb, s)
        for h in range(heads):
            query = queries[h]
            qf = query.astype(F32)
            norm = lax.rsqrt(jnp.sum(qf * qf, axis=1, keepdims=True) + 1e-06) * depth ** (-0.5)
            mixing = dot(query, keys[h], NT) * norm * fade[s, h]
            m_hi, m_lo = split(mixing)
            wu_hi, wu_lo = split(wu[s, h])
            mixed = dot(cat((m_hi, m_lo), 1), cat((wu_hi, wu_hi), 0)) + dot(m_hi, wu_lo)
            near = grow[s, h] * (qf * norm) - mixed[:, :depth]
            reach[s, h] = near
            local[s, h] = mixed[:, depth:]

        @pl.when(s > 0)
        def _():
            for h in range(heads):
                joined = mm_nt(reach[s, h], prefix[s, h])
                reach[s, h] = joined[:, :depth]
                local[s, h] += joined[:, depth:]

        return carry

    @pl.when(place > steps // 2)
    def _():
        lax.fori_loop(0, n, local_step, 0)

    cuts = chain_send.shape[1]
    rows_cut = depth // cuts

    def onward(h, c):
        return pltpu.make_async_remote_copy(
            src_ref=state_out.at[h, pl.ds(c * rows_cut, rows_cut)],
            dst_ref=state_in.at[h, pl.ds(c * rows_cut, rows_cut)],
            send_sem=chain_send.at[h, c],
            recv_sem=chain_recv.at[h, c],
            device_id={"seq": after},
            device_id_type=MESH,
        )

    @pl.when(place == 0)
    def _():
        for h in range(heads):
            state_in[h] = jnp.zeros((depth, depth), F32)
            state_out[h] = slab[h, depth:]
            for c in range(cuts):
                onward(h, c).start()

    @pl.when(place > 0)
    def _():
        for h in range(heads):
            right = rhs_square(slab[h, :depth])
            for c in range(cuts):
                piece = pl.ds(c * rows_cut, rows_cut)
                onward(h, c).wait_recv()
                state_out[h, piece] = (
                    mm(lhs_pair(state_in[h, piece]), right)
                    + slab[h, pl.ds(depth + c * rows_cut, rows_cut)]
                )

                @pl.when(place < steps - 1)
                def _():
                    onward(h, c).start()

    @pl.when(place <= steps // 2)
    def _():
        lax.fori_loop(0, n, local_step, 0)

    pltpu.make_async_copy(gain_hbm, gain_ref, gain_sem).wait()
    gain = gain_ref[...]

    def finish(d, carry):
        s = partner(me, d, n)
        wait_for(5, d)
        gates = heads_of(gb, s)
        for h in range(heads):
            result = local[s, h] + mm_nt(reach[s, h], state_in[h])
            scale = lax.rsqrt(jnp.mean(result * result, axis=1, keepdims=True) + 1e-06)
            gate = gates[h].astype(F32)
            gated = result * scale * gain * (gate / (1.0 + jnp.exp(-gate)))
            out_ref[h, pl.ds(pl.multiple_of(s * length, length), length), :] = gated.astype(BF16)
        return carry

    lax.fori_loop(0, n, finish, 0)

    for t in range(kinds):
        for d in range(1, n):
            remote(t, d).wait_send()

    @pl.when(place < steps - 1)
    def _():
        for h in range(heads):
            for c in range(cuts):
                onward(h, c).wait_send()


def body(n, steps, queries, keys, values, beta, log_decay, out_gate, norm_gain):
    length, all_heads, depth = keys.shape
    heads = all_heads // n

    cuts = 2 if depth % 16 == 0 else 1

    def grouped(x):
        return x.reshape(length, n, heads, depth)

    def rows_of(x):
        return jnp.transpose(x).reshape(n, heads, length)

    raw = (n, length, heads, depth)
    big = (n, heads, length, depth)
    tall = (n, heads, 2 * depth, depth)
    out = pl.pallas_call(
        functools.partial(kernel, n, steps, heads),
        out_shape=jax.ShapeDtypeStruct((heads, n * length, depth), BF16),
        in_specs=[pl.BlockSpec(memory_space=pl.ANY)] * 7,
        out_specs=pl.BlockSpec(memory_space=pltpu.VMEM),
        scratch_shapes=[
            pltpu.VMEM((n, heads, length), F32),
            pltpu.VMEM((n, heads, length), F32),
            pltpu.VMEM(raw, BF16),
            pltpu.VMEM(raw, BF16),
            pltpu.VMEM(raw, BF16),
            pltpu.VMEM(raw, BF16),
            pltpu.VMEM((1, depth), F32),
            pltpu.VMEM((n, heads, length, length), F32),
            pltpu.VMEM(big, F32),
            pltpu.VMEM(big, F32),
            pltpu.VMEM((n, heads, length, 2 * length), BF16),
            pltpu.VMEM((n, heads, length, 2 * depth), F32),
            pltpu.VMEM(tall, F32),
            pltpu.VMEM(tall, F32),
            pltpu.VMEM((heads, 2 * depth, depth), F32),
            pltpu.VMEM(big, F32),
            pltpu.VMEM(big, F32),
            pltpu.VMEM((heads, depth, depth), F32),
            pltpu.VMEM((heads, depth, depth), F32),
            pltpu.SemaphoreType.DMA((6, n)),
            pltpu.SemaphoreType.DMA((6, n)),
            pltpu.SemaphoreType.DMA((heads, cuts)),
            pltpu.SemaphoreType.DMA((heads, cuts)),
            pltpu.SemaphoreType.DMA,
        ],
        compiler_params=pltpu.CompilerParams(
            collective_id=0, has_side_effects=True, vmem_limit_bytes=67043328
        ),
    )(
        rows_of(beta),
        rows_of(log_decay),
        grouped(keys),
        grouped(values),
        grouped(queries),
        grouped(out_gate),
        norm_gain[None, :],
    )
    return jnp.transpose(out, (1, 0, 2))


def solution(mesh):
    return jax.shard_map(
        functools.partial(body, mesh.shape["head"], mesh.shape["seq"]),
        mesh=mesh,
        in_specs=(
            P(("seq", "head"), None, None),
            P(("seq", "head"), None, None),
            P(("seq", "head"), None, None),
            P(("seq", "head"), None),
            P(("seq", "head"), None),
            P(("seq", "head"), None, None),
            P(),
        ),
        out_specs=P("seq", "head", None),
        check_vma=False,
    )
```

time: 47 us -> 37.6 us (0.80)
  Pallas kernels: 40.6 us -> 35.2 us
  local copies, waits for them, and re-layouts: 5.3 us -> 2.24 us
  other arithmetic: 0.72 us -> 0 us
    pallas_call x1, Pallas kernels: 40.6 us -> 35.2 us  [body(): pl.pallas_call(functools.partial(kernel, n, steps, heads), out_shape=jax....]
    unnamed x12 -> x0, local copies, waits for them, and re-layouts: 4.1 us -> none
    transpose x1, local copies, waits for them, and re-layouts: 1.2 us -> 2.24 us  [body(): return jnp.transpose(out, (1, 0, 2))]
    concatenate x1 -> x0, other arithmetic: 0.72 us -> none  [body(): jnp.concatenate([rows_of(beta), rows_of(log_decay), jnp.zeros((n, padded...]
where the time goes in v2:
time: 37.6 us; the launch traced here: 37.4 us
  Pallas kernels  35.2 us (94%)
  local copies, waits for them, and re-layouts  2.24 us (6%)
    pallas_call x1, Pallas kernels, body(): pl.pallas_call(functools.partial(kernel, n, steps, heads), out_shape=jax....  35.2 us
    transpose x1, local copies, waits for them, and re-layouts, body(): return jnp.transpose(out, (1, 0, 2))  2.24 us

profile of v2, /device:TPU:27, one launch (start us, length us, event | category | flops | bytes accessed | tf_op | source)
XLA Modules:
  0.0 37.4 jit_solution(2490815831582854764)
XLA Ops:
  0.0 35.2 %shard_map.73 = bf16[4,512,128]{2,1,0:T(8,128)(2,1)} custom-call(f32[4,4,128]{2,1,0:T(4,128)} %bitcast.17, f32[4,4,128]{2,1,0:T(4,128)} %bitcast.18, bf16[128,4,4,128]{3,2,1,0:T(4,128)(2,1)} %bitcast.13, bf16[128,4,4,128]{3,2,1,0:T(4,128)(2,1)} %bitcast.14, bf16[128,4,4,128]{3,2,1,0:T(4,128)(2,1)} %bitcast.15, bf16[128,4,4,128]{3,2,1,0:T(4,128)(2,1)} %bitcast.16, ...), custom_call_target="tpu_custom_call" | custom-call | tf_op jit(solution)/shard_map/pallas_call | solution.py:323
  35.2 2.2 %copy.8 = bf16[512,4,128]{2,1,0:T(4,128)(2,1)} copy(bf16[512,4,128]{2,0,1:T(8,128)(2,1)} %bitcast.12) | data formatting | bytes 1048576 | tf_op jit(solution)/shard_map/transpose | solution.py:366

commit v3 on v2

--- a/solution.py
+++ b/solution.py
@@ -61,7 +61,7 @@
 
 def kernel(
     n, steps, heads, beta_hbm, decay_hbm, k_hbm, v_hbm, q_hbm, g_hbm, gain_hbm, out_ref,
-    betas, decays, kb, vb, qb, gb, gain_ref, fade, grow, tails, solved, wu, pairs, prefix, slab,
+    betas, decays, kb, vb, qb, gb, gain_ref, factors, fade, grow, tails, solved, wu, pairs, prefix, slab,
     local, reach, state_in, state_out, send_sem, recv_sem, chain_send, chain_recv, gain_sem,
 ):
     me = lax.axis_index("head")
@@ -173,23 +173,30 @@
 
     lax.fori_loop(0, n // group, key_step, 0)
 
-    def value_step(d, carry):
-        s = partner(me, d, n)
-        wait_for(3, d)
-        keys = heads_of(kb, s)
-        values = heads_of(vb, s)
-        for h in range(heads):
-            key, value = keys[h], values[h]
-            u = dot(solved[s, h], cat((value, value), 0))
+    def value_step(step, carry):
+        found = []
+        for j in range(group):
+            s = partner(me, step * group + j, n)
+            wait_for(3, step * group + j)
+            keys = heads_of(kb, s)
+            values = heads_of(vb, s)
+            found += [(s, h, keys[h], values[h]) for h in range(heads)]
+        us = [dot(solved[s, h], cat((value, value), 0)) for s, h, _, value in found]
+        both = [
+            cat((wu[s, h, :, :depth] * tails[s, h], u * tails[s, h]), 1)
+            for u, (s, h, _, _) in zip(us, found)
+        ]
+        moves = [
+            dot(cat(split(b), 0), cat((key, key), 0), TN)
+            for b, (_, _, key, _) in zip(both, found)
+        ]
+        for u, moved, (s, h, _, _) in zip(us, moves, found):
             wu[s, h, :, depth:] = u
-            tail = tails[s, h]
-            hi, lo = split(cat((wu[s, h, :, :depth] * tail, u * tail), 1))
-            moved = dot(cat((hi, lo), 0), cat((key, key), 0), TN)
             pairs[s, h, :depth] = grow[s, h, length - 1 :, :] * one - moved[:depth]
             pairs[s, h, depth:] = moved[depth:]
         return carry
 
-    lax.fori_loop(0, n, value_step, 0)
+    lax.fori_loop(0, n // group, value_step, 0)
 
     for h in range(heads):
         slab[h] = pairs[0, h]
@@ -232,9 +239,25 @@
 
         return carry
 
-    @pl.when(place > steps // 2)
+    @pl.when(place >= steps // 2)
     def _():
         lax.fori_loop(0, n, local_step, 0)
+
+    pltpu.make_async_copy(gain_hbm, gain_ref, gain_sem).wait()
+    gain = gain_ref[...]
+
+    def gate_step(d, carry):
+        s = partner(me, d, n)
+        wait_for(5, d)
+        gates = heads_of(gb, s)
+        for h in range(heads):
+            gate = gates[h].astype(F32)
+            factors[s, h] = gain * (gate / (1.0 + jnp.exp(-gate)))
+        return carry
+
+    @pl.when(place >= steps - 2)
+    def _():
+        lax.fori_loop(0, n, gate_step, 0)
 
     cuts = chain_send.shape[1]
     rows_cut = depth // cuts
@@ -273,22 +296,20 @@
                 def _():
                     onward(h, c).start()
 
-    @pl.when(place <= steps // 2)
+    @pl.when(place < steps // 2)
     def _():
         lax.fori_loop(0, n, local_step, 0)
 
-    pltpu.make_async_copy(gain_hbm, gain_ref, gain_sem).wait()
-    gain = gain_ref[...]
+    @pl.when(place < steps - 2)
+    def _():
+        lax.fori_loop(0, n, gate_step, 0)
 
     def finish(d, carry):
         s = partner(me, d, n)
-        wait_for(5, d)
-        gates = heads_of(gb, s)
         for h in range(heads):
             result = local[s, h] + mm_nt(reach[s, h], state_in[h])
             scale = lax.rsqrt(jnp.mean(result * result, axis=1, keepdims=True) + 1e-06)
-            gate = gates[h].astype(F32)
-            gated = result * scale * gain * (gate / (1.0 + jnp.exp(-gate)))
+            gated = result * scale * factors[s, h]
             out_ref[h, pl.ds(pl.multiple_of(s * length, length), length), :] = gated.astype(BF16)
         return carry
 
@@ -309,7 +330,7 @@
     length, all_heads, depth = keys.shape
     heads = all_heads // n
 
-    cuts = 2 if depth % 16 == 0 else 1
+    cuts = 4 if depth % 32 == 0 else 1
 
     def grouped(x):
         return x.reshape(length, n, heads, depth)
@@ -333,6 +354,7 @@
             pltpu.VMEM(raw, BF16),
             pltpu.VMEM(raw, BF16),
             pltpu.VMEM((1, depth), F32),
+            pltpu.VMEM(big, F32),
             pltpu.VMEM((n, heads, length, length), F32),
             pltpu.VMEM(big, F32),
             pltpu.VMEM(big, F32),

time: 37.6 us -> 36.5 us (0.971)
  Pallas kernels: 35.2 us -> 34.1 us
    pallas_call x1, Pallas kernels: 35.2 us -> 34.1 us  [body(): pl.pallas_call(functools.partial(kernel, n, steps, heads), out_shape=jax....]
where the time goes in v3:
time: 36.5 us; the launch traced here: 36.3 us
  Pallas kernels  34.1 us (93%)
  local copies, waits for them, and re-layouts  2.24 us (6%)
    pallas_call x1, Pallas kernels, body(): pl.pallas_call(functools.partial(kernel, n, steps, heads), out_shape=jax....  34.1 us
    transpose x1, local copies, waits for them, and re-layouts, body(): return jnp.transpose(out, (1, 0, 2))  2.24 us

profile of v3, /device:TPU:27, one launch (start us, length us, event | category | flops | bytes accessed | tf_op | source)
XLA Modules:
  0.0 36.3 jit_solution(14678264925993631660)
XLA Ops:
  0.0 34.1 %shard_map.73 = bf16[4,512,128]{2,1,0:T(8,128)(2,1)} custom-call(f32[4,4,128]{2,1,0:T(4,128)} %bitcast.17, f32[4,4,128]{2,1,0:T(4,128)} %bitcast.18, bf16[128,4,4,128]{3,2,1,0:T(4,128)(2,1)} %bitcast.13, bf16[128,4,4,128]{3,2,1,0:T(4,128)(2,1)} %bitcast.14, bf16[128,4,4,128]{3,2,1,0:T(4,128)(2,1)} %bitcast.15, bf16[128,4,4,128]{3,2,1,0:T(4,128)(2,1)} %bitcast.16, ...), custom_call_target="tpu_custom_call" | custom-call | tf_op jit(solution)/shard_map/pallas_call | solution.py:344
  34.1 2.2 %copy.8 = bf16[512,4,128]{2,1,0:T(4,128)(2,1)} copy(bf16[512,4,128]{2,0,1:T(8,128)(2,1)} %bitcast.12) | data formatting | bytes 1048576 | tf_op jit(solution)/shard_map/transpose | solution.py:388
